TPU v7x, 32 devices: a whole 2x2x4 slice. The times are simulated.
32 devices in a mesh: gx: 4 (over x, core), gy: 8 (over z, y).
Axes of the slice: x: 2, y: 2, z: 4, core: 2. Of those that a mesh axis runs over, the one named last changes fastest.
Arguments:
- base: int32 [2, 3, 65536], P(None, None, ('gx', 'gy')), may hold values from -2 to 125, as said below
- offset: float32 [2, 3, 65536], P(None, None, ('gx', 'gy')), may hold values from 0.5 to 1.5
- velocity: float32 [3, 65536], P(None, ('gx', 'gy')), may hold values from -4 to 4
- affine: float32 [9, 65536], P(None, ('gx', 'gy')), may hold values from -3 to 3
- volume: float32 [65536], P(('gx', 'gy')), may hold values from 0.8 to 1.25
- node_mask: int32 [128, 128, 128], P('gx', 'gy'), may hold values 0 or 1
- direction: int32 [65536], P(('gx', 'gy')), may hold values from 0 to 8, as said below
Outputs:
- migrated: float32 [16, 98304], P(None, ('gx', 'gy'))
Inputs may be any that keep to these rules, and one draw needn't show every extreme that they name: base[s, 0] lies in -2 to 31, base[s, 1] in -2 to 15, base[s, 2] in 0 to 125. Of one block column's rows, at most 128 carry any one direction other than 4; in every draw some block column has exactly 128 rows in some direction.
All inputs are finite; a program needn't handle non-finite values. No bound on the sum of `node_mask` on one device may be relied on, other than what follows from the above.
Results may differ from a plain program's by a relative error of at most 0.0003.
Values may be sent and summed in bfloat16 or wider, within the bound.
A program may use at most 64 MiB of HBM per device.

v0:
```python
import functools

import jax
import jax.numpy as jnp
import numpy as np
from jax import lax
from jax.experimental import pallas as pl
from jax.experimental.pallas import tpu as pltpu
from jax.sharding import PartitionSpec as P

PARTICLE_MASS = 1.0
STIFFNESS = 4.0
TIME_STEP = 0.1
GRAVITY = 3.0
MASS_FLOOR = 0.5
LANES = 128
OUTSIDE = -100

F32 = jnp.float32
BF16 = jnp.bfloat16
NT = (((1,), (1,)), ((), ()))

BLOCKS = ((0, -1), (0, 1), (-1, 0), (1, 0), (-1, -1), (-1, 1), (1, -1), (1, 1))
CORNER_ROWS = 16


def block_rows(size_x, size_y):
    counts = [2 * size_x] * 2 + [2 * size_y] * 2 + [CORNER_ROWS] * 4
    starts = [sum(counts[:place]) for place in range(8)]
    return (list(zip(starts, counts)), sum(counts))


def owner_rows(size_x, size_y):
    places, total = block_rows(size_x, size_y)
    rows = np.full(total, -1, np.int64)
    for (dx, dy), (start, _) in zip(BLOCKS, places):
        span_x = range(2) if dx else range(size_x)
        span_y = range(2) if dy else range(size_y)
        low_x = size_x - 2 if dx < 0 else 0
        low_y = size_y - 2 if dy < 0 else 0
        for x in span_x:
            for y in span_y:
                if dx and dy:
                    spot = 2 * x + y
                elif dx:
                    spot = x * size_y + y
                else:
                    spot = y * size_x + x
                rows[start + spot] = (low_x + x) * size_y + low_y + y
    return rows


def spline(frac):
    return [0.5 * (1.5 - frac) ** 2, 0.75 - (frac - 1.0) ** 2, 0.5 * (frac - 0.5) ** 2]


def pick(place, values):
    return jnp.where(
        place == 0,
        values[0],
        jnp.where(place == 1, values[1], jnp.where(place == 2, values[2], 0.0)),
    )


def weights_of(offsets):
    weights = [spline(offsets[axis : axis + 1]) for axis in range(3)]
    slopes = [
        [weights[axis][node] * (float(node) - offsets[axis : axis + 1]) for node in range(3)]
        for axis in range(3)
    ]
    return (weights, slopes)


def rows_iota(count):
    return lax.broadcasted_iota(jnp.int32, (count, 1), 0)


def build(bases, weights, slopes, size_x, size_y, tab, xw, xs, yw, ys):
    width = bases.shape[1]
    from_x = bases[0:1] + 2
    from_y = bases[1:2] + 2
    edge = rows_iota(8)
    for size, start, axis, plain, slope in ((size_x, from_x, 0, xw, xs), (size_y, from_y, 1, yw, ys)):
        place = rows_iota(size) + 2 - start
        plain[0:size] = pick(place, weights[axis])
        slope[0:size] = pick(place, slopes[axis])
        coord = jnp.where(edge < 2, edge, jnp.where(edge < 4, edge + size, OUTSIDE))
        place = coord - start
        plain[size : size + 8] = pick(place, weights[axis])
        slope[size : size + 8] = pick(place, slopes[axis])

    def put(row, count, wx, sx, wy, sy):
        tab[row : row + count, 0:width] = (wx * wy).astype(BF16)
        tab[row : row + count, width : 2 * width] = (sx * wy).astype(BF16)
        tab[row : row + count, 2 * width : 3 * width] = (wx * sy).astype(BF16)

    places, margin = block_rows(size_x, size_y)
    wide_w, wide_s = (xw[0:size_x], xs[0:size_x])
    for k in range(4):
        one = slice(size_y + k, size_y + k + 1)
        put(k * size_x, size_x, wide_w, wide_s, yw[one], ys[one])
    tall_w, tall_s = (yw[0:size_y], ys[0:size_y])
    for k in range(4):
        one = slice(size_x + k, size_x + k + 1)
        put(places[2][0] + k * size_y, size_y, xw[one], xs[one], tall_w, tall_s)
    spot = rows_iota(CORNER_ROWS)
    for k in range(4):
        high_x, high_y = (k // 2, k % 2)
        coord_x = jnp.where(spot < 4, (spot >> 1) + high_x * (size_x + 2), OUTSIDE)
        coord_y = jnp.where(spot < 4, (spot & 1) + high_y * (size_y + 2), OUTSIDE)
        place_x = coord_x - from_x
        place_y = coord_y - from_y
        put(
            places[4 + k][0],
            CORNER_ROWS,
            pick(place_x, weights[0]),
            pick(place_x, slopes[0]),
            pick(place_y, weights[1]),
            pick(place_y, slopes[1]),
        )
    for x in range(size_x):
        one = slice(x, x + 1)
        put(margin + x * size_y, size_y, xw[one], xs[one], tall_w, tall_s)


def depth_tables(bases, weights, slopes, depth):
    place = rows_iota(depth) - bases[2:3]
    return (pick(place, weights[2]), pick(place, slopes[2]))


def scatter_chunk(bases, offsets, vel, aff, vol, sizes, tab, right, tables, total):
    size_x, size_y, depth = sizes
    _, edge = block_rows(size_x, size_y)
    width = bases.shape[1]
    weights, slopes = weights_of(offsets)
    build(bases, weights, slopes, size_x, size_y, tab, *tables)
    depth_w, depth_s = depth_tables(bases, weights, slopes, depth)
    stress = -STIFFNESS * (vol - 1.0)

    def entry(i, j):
        value = PARTICLE_MASS * aff[3 * i + j]
        return value + stress if i == j else value

    zeros = jnp.zeros((depth, 2 * width), BF16)
    right[0:depth, 0:width] = (depth_w * PARTICLE_MASS).astype(BF16)
    right[0:depth, width : 3 * width] = zeros
    for i in range(3):
        rows = slice((i + 1) * depth, (i + 2) * depth)
        moment = PARTICLE_MASS * vel[i]
        right[rows, 0:width] = (depth_w * moment + depth_s * entry(i, 2)).astype(BF16)
        right[rows, width : 2 * width] = (depth_w * entry(i, 0)).astype(BF16)
        right[rows, 2 * width : 3 * width] = (depth_w * entry(i, 1)).astype(BF16)
    total[0:edge] += lax.dot_general(tab[0:edge], right[...], NT, preferred_element_type=F32)


def gather_chunk(bases, offsets, vol, sizes, wide, tab, result, tables):
    size_x, size_y, depth = sizes
    width = bases.shape[1]
    weights, slopes = weights_of(offsets)
    build(bases, weights, slopes, size_x, size_y, tab, *tables)
    depth_w, depth_s = depth_tables(bases, weights, slopes, depth)
    result[...] = jnp.dot(wide[...], tab[...], preferred_element_type=F32)
    vel, aff = ([], [None] * 9)
    for i in range(3):
        rows = slice(i * depth, (i + 1) * depth)
        plain = result[rows, 0:width]
        vel.append(jnp.sum(plain * depth_w, 0, keepdims=True))
        aff[3 * i + 2] = 4.0 * jnp.sum(plain * depth_s, 0, keepdims=True)
        aff[3 * i] = 4.0 * jnp.sum(result[rows, width : 2 * width] * depth_w, 0, keepdims=True)
        aff[3 * i + 1] = 4.0 * jnp.sum(
            result[rows, 2 * width : 3 * width] * depth_w, 0, keepdims=True
        )
    vol = vol * (1.0 + TIME_STEP * (aff[0] + aff[4] + aff[8]))
    return (vel, aff, vol)


def take_rows(ref, lanes, count):
    return [ref[k : k + 1, lanes] for k in range(count)]


def first_kernel(sizes, counts, chunk, base, offset, vel, aff, vol, mask, place_in, take_out, wide, tab, right, total, xw, xs, yw, ys, *remote):
    greet(counts)
    total[...] = jnp.zeros_like(total)

    def body(step, carry):
        lanes = pl.ds(pl.multiple_of(step * chunk, chunk), chunk)
        scatter_chunk(
            base[:, 0, lanes], offset[:, 0, lanes], take_rows(vel, lanes, 3),
            take_rows(aff, lanes, 9), vol[:, lanes], sizes, tab.at[step], right.at[step],
            (xw, xs, yw, ys), total,
        )
        return carry

    lax.fori_loop(0, vel.shape[1] // chunk, body, 0)
    exchange(sizes, counts, mask, place_in, take_out, wide, tab, right, total, *remote)


def middle_kernel(sizes, counts, chunk, base, offset, vol, before, mask, place_in, take_out, wide, vol_out, seen, result, tab, right, total, xw, xs, yw, ys, *remote):
    greet(counts)
    total[...] = jnp.zeros_like(total)

    def body(step, carry):
        lanes = pl.ds(pl.multiple_of(step * chunk, chunk), chunk)
        vel, aff, ratio = gather_chunk(
            base[:, 0, lanes], offset[:, 0, lanes], vol[:, lanes], sizes, before, seen, result,
            (xw, xs, yw, ys),
        )
        vol_out[:, lanes] = ratio
        scatter_chunk(
            base[:, 1, lanes], offset[:, 1, lanes], vel, aff, ratio, sizes, tab.at[step],
            right.at[step], (xw, xs, yw, ys), total,
        )
        return carry

    lax.fori_loop(0, vol.shape[1] // chunk, body, 0)
    exchange(sizes, counts, mask, place_in, take_out, wide, tab, right, total, *remote)


def last_kernel(sizes, chunk, capacity, counts, base, offset, vol, wide, direction, out, tab, result, state, slots, xw, xs, yw, ys, buckets, got, sends, recvs):
    greet(counts)
    tables = (xw, xs, yw, ys)
    size_x, size_y, _ = sizes
    count_x, count_y = counts
    index_x = lax.axis_index("gx")
    index_y = lax.axis_index("gy")
    rows = vol.shape[1]

    def route(code):
        step_x = jnp.where(code < 3, -1, jnp.where(code > 5, 1, 0))
        step_y = code - 3 * step_x - 4
        to_x = step_x + index_x
        to_y = step_y + index_y
        inside = (to_x >= 0) & (to_x < count_x) & (to_y >= 0) & (to_y < count_y)
        return (
            jnp.where(inside, code, 4),
            jnp.where(inside, step_x, 0),
            jnp.where(inside, step_y, 0),
        )

    def body(step, carry):
        lanes = pl.ds(pl.multiple_of(step * chunk, chunk), chunk)
        bases = base[:, 1, lanes]
        offsets = offset[:, 1, lanes]
        vel, aff, ratio = gather_chunk(
            bases, offsets, vol[:, lanes], sizes, wide, tab, result, tables
        )
        moving, step_x, step_y = route(direction[:, lanes])
        shift = (step_x * size_x, step_y * size_y, None)
        for axis in range(3):
            spot = bases[axis : axis + 1].astype(F32) + offsets[axis : axis + 1]
            spot = spot + TIME_STEP * vel[axis]
            if shift[axis] is not None:
                spot = spot - shift[axis].astype(F32)
            state[axis : axis + 1, lanes] = spot
            state[3 + axis : 4 + axis, lanes] = vel[axis]
        for k in range(9):
            state[6 + k : 7 + k, lanes] = aff[k]
        state[15:16, lanes] = ratio
        out[:, lanes] = jnp.where(moving == 4, state[:, lanes], 0.0)
        return carry

    lax.fori_loop(0, rows // chunk, body, 0)

    parts = rows // LANES
    place = rows_iota(8)
    codes = jnp.where(place < 4, place, place + 1)
    hits = []
    for part in range(parts):
        moving, _, _ = route(direction[:, part * LANES : (part + 1) * LANES])
        hits.append(jnp.where(moving == codes, 1.0, 0.0))
    above = lax.broadcasted_iota(jnp.int32, (LANES, 2 * LANES), 0)
    along = lax.broadcasted_iota(jnp.int32, (LANES, 2 * LANES), 1)
    summer = jnp.where(above <= along, 1.0, 0.0).astype(BF16)
    sums = jnp.dot(jnp.concatenate(hits, 0).astype(BF16), summer, preferred_element_type=F32)
    before = (place * capacity).astype(F32)
    before = jnp.broadcast_to(before, (8, LANES))
    for part in range(parts):
        mine = slice(part * 8, (part + 1) * 8)
        slot = jnp.sum(hits[part] * (sums[mine, 0:LANES] + before), 0, keepdims=True) - 1.0
        slots[:, part * LANES : (part + 1) * LANES] = slot.astype(jnp.int32)
        before = before + sums[mine, LANES:]

    value = state[...]
    high = value.astype(BF16)
    rest = value - high.astype(F32)
    middle = rest.astype(BF16)
    low = (rest - middle.astype(F32)).astype(BF16)
    split = jnp.concatenate([high, middle, low], 0)
    for k in range(8):
        chosen = slots[...] - k * capacity == rows_iota(capacity)
        chosen = jnp.where(chosen, 1.0, 0.0).astype(BF16)
        packed = lax.dot_general(split, chosen, NT, preferred_element_type=F32)
        buckets[k] = packed[0:16] + packed[16:32] + packed[32:48]
    migrate(counts, buckets, out, got, sends, recvs)


def neighbour(counts, dx, dy):
    to_x = lax.axis_index("gx") + dx
    to_y = lax.axis_index("gy") + dy
    exists = (to_x >= 0) & (to_x < counts[0]) & (to_y >= 0) & (to_y < counts[1])
    return (exists, {"gx": to_x, "gy": to_y})


def greet(counts):
    barrier = pltpu.get_barrier_semaphore()
    for dx, dy in BLOCKS:
        exists, where = neighbour(counts, dx, dy)

        @pl.when(exists)
        def _():
            pl.semaphore_signal(
                barrier, inc=1, device_id=where, device_id_type=pl.DeviceIdType.MESH
            )


def await_peers(counts):
    barrier = pltpu.get_barrier_semaphore()
    peers = 0
    for dx, dy in BLOCKS:
        exists, _ = neighbour(counts, dx, dy)
        peers = peers + exists.astype(jnp.int32)
    pl.semaphore_wait(barrier, peers)


def transfers(counts, sign, source, target, send_sems, recv_sems):
    copies = []
    for k, (dx, dy) in enumerate(BLOCKS):
        exists, where = neighbour(counts, sign * dx, sign * dy)
        copy = pltpu.make_async_remote_copy(
            src_ref=source(k),
            dst_ref=target(k),
            send_sem=send_sems.at[k],
            recv_sem=recv_sems.at[k],
            device_id=where,
            device_id_type=pl.DeviceIdType.MESH,
        )
        comes, _ = neighbour(counts, -sign * dx, -sign * dy)
        copies.append((exists, comes, copy))
    return copies


def start_all(copies, target):
    for exists, _, copy in copies:
        pl.when(exists)(copy.start)
    for k, (_, comes, _) in enumerate(copies):

        @pl.when(jnp.logical_not(comes))
        def _():
            view = target(k)
            view[...] = jnp.zeros(view.shape, view.dtype)


def wait_all(copies):
    for _, comes, copy in copies:
        pl.when(comes)(copy.wait_recv)
    for exists, _, copy in copies:
        pl.when(exists)(copy.wait_send)


def pack_corners(value, channels, depth, spread):
    for k in range(4):
        for c in range(channels):
            spread[k * CORNER_ROWS + 4 * c : k * CORNER_ROWS + 4 * c + 4, :] = value(
                slice(k * CORNER_ROWS, k * CORNER_ROWS + 4), slice(c * depth, (c + 1) * depth)
            )


def unpack_corners(spread, channels, depth, square):
    square[...] = jnp.zeros_like(square)
    for k in range(4):
        for c in range(channels):
            square[
                k * CORNER_ROWS : k * CORNER_ROWS + 4, c * depth : (c + 1) * depth
            ] = spread[k * CORNER_ROWS + 4 * c : k * CORNER_ROWS + 4 * c + 4, :]


def exchange(sizes, counts, mask, place_in, take_out, wide, tab, right, total, margins, corners, got, got_corners, sent, sent_corners, halo, halo_corners, spread, square, speed, drawn, sends, recvs, sends_b, recvs_b):
    size_x, size_y, depth = sizes
    places, edge = block_rows(size_x, size_y)
    inner = places[4][0]

    def views(sides, tiles):
        def view(k):
            if k < 4:
                return sides.at[pl.ds(places[k][0], places[k][1])]
            return tiles.at[pl.ds((k - 4) * CORNER_ROWS, CORNER_ROWS)]

        return view

    margins[...] = total[0:inner].astype(BF16)

    def corner_of(rows, lanes):
        return total[inner + rows.start : inner + rows.stop, lanes]

    pack_corners(corner_of, 4, depth, spread)
    corners[...] = spread[...].astype(BF16)
    await_peers(counts)
    arriving = views(got, got_corners)
    copies = transfers(counts, 1, views(margins, corners), arriving, sends, recvs)
    start_all(copies, arriving)

    def body(step, carry):
        total[edge:] += lax.dot_general(
            tab[step, edge:], right[step], NT, preferred_element_type=F32
        )
        return carry

    lax.fori_loop(0, tab.shape[0], body, 0)
    wait_all(copies)
    spread[...] = got_corners[...].astype(F32)
    unpack_corners(spread, 4, depth, square)
    received = jnp.concatenate([got[...], square[...].astype(BF16)], 0)
    full = total[edge:] + jnp.dot(place_in[...], received, preferred_element_type=F32)
    mass = jnp.maximum(full[:, 0:depth], MASS_FLOOR)
    keep = (1 - mask[...]).astype(F32)
    for axis in range(3):
        value = full[:, (axis + 1) * depth : (axis + 2) * depth] / mass
        if axis == 2:
            value = value - TIME_STEP * GRAVITY
        speed[:, axis * depth : (axis + 1) * depth] = (value * keep).astype(BF16)
    drawn[...] = jnp.dot(take_out[...], speed[...], preferred_element_type=F32)
    sent[...] = drawn[0:inner].astype(BF16)

    def drawn_corner(rows, lanes):
        return drawn[inner + rows.start : inner + rows.stop, lanes]

    pack_corners(drawn_corner, 3, depth, spread)
    sent_corners[...] = spread[...].astype(BF16)
    arriving = views(halo, halo_corners)
    copies = transfers(counts, -1, views(sent, sent_corners), arriving, sends_b, recvs_b)
    start_all(copies, arriving)
    for axis in range(3):
        lanes = slice(axis * depth, (axis + 1) * depth)
        wide[lanes, edge:] = speed[:, lanes].astype(F32).T.astype(BF16)
    wait_all(copies)
    spread[...] = halo_corners[...].astype(F32)
    unpack_corners(spread, 3, depth, square)
    for axis in range(3):
        lanes = slice(axis * depth, (axis + 1) * depth)
        outer = jnp.concatenate([halo[:, lanes].astype(F32), square[:, lanes]], 0)
        wide[lanes, 0:edge] = outer.T.astype(BF16)


def migrate(counts, buckets, out, got, sends, recvs):
    capacity = buckets.shape[2]
    rows = out.shape[1] - 8 * capacity
    order = [0, 1, 2, 3, 5, 6, 7, 8]
    slot_of = [order.index(3 * (dx + 1) + dy + 1) for dx, dy in BLOCKS]

    def views(ref):
        return lambda k: ref.at[slot_of[k]]

    await_peers(counts)
    copies = transfers(counts, 1, views(buckets), views(got), sends, recvs)
    start_all(copies, views(got))
    wait_all(copies)
    for k in range(8):
        out[:, rows + k * capacity : rows + (k + 1) * capacity] = got[k]


def vmem(count):
    return [pl.BlockSpec(memory_space=pltpu.VMEM)] * count


def per_device(counts, base, offset, velocity, affine, volume, node_mask, direction):
    sizes = node_mask.shape
    size_x, size_y, depth = sizes
    rows = velocity.shape[1]
    capacity = rows // 16
    chunk = min(rows, 512)
    _, edge = block_rows(size_x, size_y)
    cells = size_x * size_y
    all_rows = edge + cells
    base = jnp.swapaxes(base, 0, 1)
    offset = jnp.swapaxes(offset, 0, 1)
    volume = volume.reshape(1, rows)
    direction = direction.reshape(1, rows)
    mask = node_mask.reshape(cells, depth)
    owners = owner_rows(size_x, size_y)
    choose = (owners[:, None] == np.arange(cells)[None]).astype(np.float32)
    take_out = jnp.asarray(choose, BF16)
    place_in = jnp.asarray(choose.T, BF16)

    inner = edge - 4 * CORNER_ROWS
    steps = rows // chunk
    seen = pltpu.VMEM((all_rows, 3 * chunk), BF16)
    result = pltpu.VMEM((3 * depth, 3 * chunk), F32)
    tables = [pltpu.VMEM((size_x + 8, chunk), F32)] * 2 + [pltpu.VMEM((size_y + 8, chunk), F32)] * 2
    spread = [
        pltpu.VMEM((steps, all_rows, 3 * chunk), BF16),
        pltpu.VMEM((steps, 4 * depth, 3 * chunk), BF16),
        pltpu.VMEM((all_rows, 4 * depth), F32),
    ] + tables
    remote = [
        pltpu.VMEM((inner, 4 * depth), BF16),
        pltpu.VMEM((4 * CORNER_ROWS, depth), BF16),
        pltpu.VMEM((inner, 4 * depth), BF16),
        pltpu.VMEM((4 * CORNER_ROWS, depth), BF16),
        pltpu.VMEM((inner, 3 * depth), BF16),
        pltpu.VMEM((4 * CORNER_ROWS, depth), BF16),
        pltpu.VMEM((inner, 3 * depth), BF16),
        pltpu.VMEM((4 * CORNER_ROWS, depth), BF16),
        pltpu.VMEM((4 * CORNER_ROWS, depth), F32),
        pltpu.VMEM((4 * CORNER_ROWS, 4 * depth), F32),
        pltpu.VMEM((cells, 3 * depth), BF16),
        pltpu.VMEM((edge, 3 * depth), F32),
    ] + [pltpu.SemaphoreType.DMA((8,))] * 4
    wide_out = jax.ShapeDtypeStruct((3 * depth, all_rows), BF16)

    def params(number):
        return pltpu.CompilerParams(
            collective_id=number, has_side_effects=True, vmem_limit_bytes=56 * 1024 * 1024
        )

    wide = pl.pallas_call(
        functools.partial(first_kernel, sizes, counts, chunk),
        out_shape=wide_out,
        in_specs=vmem(8),
        out_specs=vmem(1)[0],
        scratch_shapes=spread + remote,
        compiler_params=params(0),
        name="scatter",
    )(base, offset, velocity, affine, volume, mask, place_in, take_out)
    wide, volume = pl.pallas_call(
        functools.partial(middle_kernel, sizes, counts, chunk),
        out_shape=[wide_out, jax.ShapeDtypeStruct((1, rows), F32)],
        in_specs=vmem(7),
        out_specs=vmem(2),
        scratch_shapes=[seen, result] + spread + remote,
        compiler_params=params(1),
        name="gather_scatter",
    )(base, offset, volume, wide, mask, place_in, take_out)
    return pl.pallas_call(
        functools.partial(last_kernel, sizes, chunk, capacity, counts),
        out_shape=jax.ShapeDtypeStruct((16, rows + 8 * capacity), F32),
        in_specs=vmem(5),
        out_specs=vmem(1)[0],
        scratch_shapes=[seen, result, pltpu.VMEM((16, rows), F32), pltpu.VMEM((1, rows), jnp.int32)]
        + tables
        + [pltpu.VMEM((8, 16, capacity), F32)] * 2
        + [pltpu.SemaphoreType.DMA((8,))] * 2,
        compiler_params=params(2),
        name="gather_pack",
    )(base, offset, volume, wide, direction)


def solution(mesh):
    counts = (mesh.shape["gx"], mesh.shape["gy"])
    placed = (
        P(None, None, ("gx", "gy")),
        P(None, None, ("gx", "gy")),
        P(None, ("gx", "gy")),
        P(None, ("gx", "gy")),
        P(("gx", "gy")),
        P("gx", "gy", None),
        P(("gx", "gy")),
    )
    return jax.shard_map(
        functools.partial(per_device, counts),
        mesh=mesh,
        in_specs=placed,
        out_specs=P(None, ("gx", "gy")),
        check_vma=False,
    )
```

profile of v0, /device:TPU:0, one launch (start us, length us, event | category | flops | bytes accessed | tf_op | source)
XLA Modules:
  0.0 52.3 jit_solution(9166543919780105284)
XLA Ops:
  0.0 17.0 %scatter.1.before = bf16[384,768]{1,0:T(8,128)(2,1)} custom-call(s32[3,2,2048]{2,1,0:T(2,128)} %bitcast.7, f32[3,2,2048]{2,1,0:T(2,128)} %bitcast.10, f32[3,2048]{1,0:T(4,128)} %vel.1, f32[9,2048]{1,0:T(8,128)} %aff.1, f32[1,2048]{1,0:T(1,128)} %bitcast.13, s32[512,128]{1,0:T(8,128)} %bitcast.5, bf16[512,256]{1,0:T(8,128)(2,1)} %constant.5.clone.place_in, ...), custom_call_target="tpu_custom_call" | custom-call | tf_op jit(solution)/shard_map/scatter/pallas_call | solution.py:515
  17.0 20.7 %gather_scatter.1 = (bf16[384,768]{1,0:T(8,128)(2,1)}, f32[1,2048]{1,0:T(1,128)}) custom-call(s32[3,2,2048]{2,1,0:T(2,128)} %bitcast.8, f32[3,2,2048]{2,1,0:T(2,128)} %bitcast.11, f32[1,2048]{1,0:T(1,128)} %bitcast.14, bf16[384,768]{1,0:T(8,128)(2,1)} %scatter.1.before, s32[512,128]{1,0:T(8,128)} %bitcast.6, bf16[512,256]{1,0:T(8,128)(2,1)} %constant.5.clone.place_in, ...), custom_call_target="tpu_custom_call" | custom-call | tf_op jit(solution)/shard_map/gather_scatter/pallas_call | solution.py:524
  37.7 13.0 %gather_pack.1 = f32[16,3072]{1,0:T(8,128)} custom-call(s32[3,2,2048]{2,1,0:T(2,128)} %bitcast.9, f32[3,2,2048]{2,1,0:T(2,128)} %bitcast.12, f32[1,2048]{1,0:T(1,128)} %get-tuple-element.7.vol, bf16[384,768]{1,0:T(8,128)(2,1)} %get-tuple-element.8.wide, s32[1,2048]{1,0:T(1,128)} %bitcast.15), custom_call_target="tpu_custom_call" | custom-call | tf_op jit(solution)/shard_map/gather_pack/pallas_call | solution.py:533
  50.7 1.6 %copy.11 = f32[16,3072]{1,0:T(8,128)} copy(f32[16,3072]{1,0:T(8,128)} %gather_pack.1) | data formatting | bytes 393216
where the time goes:
time: 52.5 us; the launch traced here: 52.3 us
  Pallas kernels  50.7 us (97%)
  local copies, waits for them, and re-layouts  1.62 us (3%)
    pallas_call x1, Pallas kernels, per_device(): pl.pallas_call(functools.partial(middle_kernel, sizes, counts, chunk), ou...  20.7 us
    pallas_call x1, Pallas kernels, per_device(): pl.pallas_call(functools.partial(first_kernel, sizes, counts, chunk), out...  17 us
    pallas_call x1, Pallas kernels, per_device(): pl.pallas_call(functools.partial(last_kernel, sizes, chunk, capacity, cou...  13 us
    unnamed x1, local copies, waits for them, and re-layouts  1.62 us

commit v1 on v0

v1 whole, which is shorter than its diff:
```python
import functools

import jax
import jax.numpy as jnp
from jax import lax
from jax.experimental import pallas as pl
from jax.experimental.pallas import tpu as pltpu
from jax.sharding import PartitionSpec as P

PARTICLE_MASS = 1.0
STIFFNESS = 4.0
TIME_STEP = 0.1
GRAVITY = 3.0
MASS_FLOOR = 0.5
LANES = 128
OUTSIDE = -100

F32 = jnp.float32
BF16 = jnp.bfloat16
NT = (((1,), (1,)), ((), ()))

SIDES = ((0, -1), (0, 1), (-1, 0), (1, 0))
CORNERS = ((-1, -1), (-1, 1), (1, -1), (1, 1))
BLOCKS = SIDES + CORNERS
ISSUE = (4, 5, 6, 7, 0, 1, 2, 3)
CORNER_ROWS = 16


class Sizes:
    def __init__(self, size_x, size_y, depth, rows, chunk):
        self.x, self.y, self.depth, self.rows, self.chunk = size_x, size_y, depth, rows, chunk
        self.steps = rows // chunk
        self.cells = size_x * size_y
        counts = [2 * size_x] * 2 + [2 * size_y] * 2
        self.sides = [(sum(counts[:k]), counts[k]) for k in range(4)]
        self.corner = sum(counts)
        self.used = self.corner + 16
        self.edge = -(-self.used // 256) * 256


def spline(frac):
    return [0.5 * (1.5 - frac) ** 2, 0.75 - (frac - 1.0) ** 2, 0.5 * (frac - 0.5) ** 2]


def pick(place, values):
    return jnp.where(
        place == 0,
        values[0],
        jnp.where(place == 1, values[1], jnp.where(place == 2, values[2], 0.0)),
    )


def weights_of(offsets):
    weights = [spline(offsets[axis : axis + 1]) for axis in range(3)]
    slopes = [
        [weights[axis][node] * (float(node) - offsets[axis : axis + 1]) for node in range(3)]
        for axis in range(3)
    ]
    return (weights, slopes)


def rows_iota(count):
    return lax.broadcasted_iota(jnp.int32, (count, 1), 0)


def build(sz, bases, offsets, tab, tables, depth_w, depth_s):
    xw, xs, yw, ys = tables
    width = bases.shape[1]
    weights, slopes = weights_of(offsets)
    from_x = bases[0:1] + 2
    from_y = bases[1:2] + 2
    edge = rows_iota(8)
    for size, start, axis, plain, slope in ((sz.x, from_x, 0, xw, xs), (sz.y, from_y, 1, yw, ys)):
        place = rows_iota(size) + 2 - start
        plain[0:size] = pick(place, weights[axis])
        slope[0:size] = pick(place, slopes[axis])
        coord = jnp.where(edge < 2, edge, jnp.where(edge < 4, edge + size, OUTSIDE))
        place = coord - start
        plain[size : size + 8] = pick(place, weights[axis])
        slope[size : size + 8] = pick(place, slopes[axis])

    def put(row, count, wx, sx, wy, sy):
        tab[row : row + count, 0:width] = (wx * wy).astype(BF16)
        tab[row : row + count, width : 2 * width] = (sx * wy).astype(BF16)
        tab[row : row + count, 2 * width : 3 * width] = (wx * sy).astype(BF16)

    wide_w, wide_s = (xw[0 : sz.x], xs[0 : sz.x])
    tall_w, tall_s = (yw[0 : sz.y], ys[0 : sz.y])
    for k in range(4):
        one = slice(sz.y + k, sz.y + k + 1)
        put(k * sz.x, sz.x, wide_w, wide_s, yw[one], ys[one])
    for k in range(4):
        one = slice(sz.x + k, sz.x + k + 1)
        put(sz.sides[2][0] + k * sz.y, sz.y, xw[one], xs[one], tall_w, tall_s)
    spot = rows_iota(16)
    coord_x = ((spot >> 1) & 1) + (spot >> 3) * (sz.x + 2)
    coord_y = (spot & 1) + ((spot >> 2) & 1) * (sz.y + 2)
    place_x = coord_x - from_x
    place_y = coord_y - from_y
    put(
        sz.corner,
        16,
        pick(place_x, weights[0]),
        pick(place_x, slopes[0]),
        pick(place_y, weights[1]),
        pick(place_y, slopes[1]),
    )
    for y in range(sz.y):
        one = slice(y, y + 1)
        put(sz.edge + y * sz.x, sz.x, wide_w, wide_s, yw[one], ys[one])
    place = rows_iota(sz.depth) - bases[2:3]
    depth_w[...] = pick(place, weights[2])
    depth_s[...] = pick(place, slopes[2])


def build_right(sz, vel, aff, vol, depth_w, depth_s, right):
    depth = sz.depth
    width = vol.shape[1]
    stress = -STIFFNESS * (vol - 1.0)

    def entry(i, j):
        value = PARTICLE_MASS * aff[3 * i + j]
        return value + stress if i == j else value

    plain = depth_w[...]
    slope = depth_s[...]
    right[0:depth, 0:width] = (plain * PARTICLE_MASS).astype(BF16)
    for i in range(3):
        rows = slice((i + 1) * depth, (i + 2) * depth)
        moment = PARTICLE_MASS * vel[i]
        right[rows, 0:width] = (plain * moment + slope * entry(i, 2)).astype(BF16)
        right[rows, width : 2 * width] = (plain * entry(i, 0)).astype(BF16)
        right[rows, 2 * width : 3 * width] = (plain * entry(i, 1)).astype(BF16)


def reduce_depth(sz, result, depth_w, depth_s):
    width = depth_w.shape[1]

    def fold(value):
        return jnp.sum(value.reshape(sz.depth // 8, 8, width), 0)

    sums = []
    for i in range(3):
        rows = slice(i * sz.depth, (i + 1) * sz.depth)
        plain = result[rows, 0:width]
        sums.append(fold(plain * depth_w[...]))
        sums.append(fold(result[rows, width : 2 * width] * depth_w[...]))
        sums.append(fold(result[rows, 2 * width : 3 * width] * depth_w[...]))
        sums.append(fold(plain * depth_s[...]))
    return sums


def finish(sums, vol):
    vel = [jnp.sum(sums[4 * i], 0, keepdims=True) for i in range(3)]
    aff = [
        4.0 * jnp.sum(sums[4 * i + 1 + a], 0, keepdims=True) for i in range(3) for a in range(3)
    ]
    return (vel, aff, vol * (1.0 + TIME_STEP * (aff[0] + aff[4] + aff[8])))


def neighbour(counts, dx, dy):
    to_x = lax.axis_index("gx") + dx
    to_y = lax.axis_index("gy") + dy
    exists = (to_x >= 0) & (to_x < counts[0]) & (to_y >= 0) & (to_y < counts[1])
    return (exists, {"gx": to_x, "gy": to_y})


def greet(counts):
    barrier = pltpu.get_barrier_semaphore()
    for dx, dy in BLOCKS:
        exists, where = neighbour(counts, dx, dy)

        @pl.when(exists)
        def _():
            pl.semaphore_signal(
                barrier, inc=1, device_id=where, device_id_type=pl.DeviceIdType.MESH
            )


def await_peers(counts):
    barrier = pltpu.get_barrier_semaphore()
    peers = 0
    for dx, dy in BLOCKS:
        exists, _ = neighbour(counts, dx, dy)
        peers = peers + exists.astype(jnp.int32)
    pl.semaphore_wait(barrier, peers)


def transfers(counts, sign, source, target, send_sems, recv_sems):
    copies = []
    for k, (dx, dy) in enumerate(BLOCKS):
        exists, where = neighbour(counts, sign * dx, sign * dy)
        copy = pltpu.make_async_remote_copy(
            src_ref=source(k),
            dst_ref=target(k),
            send_sem=send_sems.at[k],
            recv_sem=recv_sems.at[k],
            device_id=where,
            device_id_type=pl.DeviceIdType.MESH,
        )
        comes, _ = neighbour(counts, -sign * dx, -sign * dy)
        copies.append((exists, comes, copy))
    return copies


def start_all(copies, picked=ISSUE):
    for k in picked:
        pl.when(copies[k][0])(copies[k][2].start)


def wait_arrivals(copies, picked=ISSUE):
    for k in picked:
        pl.when(copies[k][1])(copies[k][2].wait_recv)


def wait_sends(copies):
    for exists, _, copy in copies:
        pl.when(exists)(copy.wait_send)


def clear_missing(counts, sign, target):
    for k, (dx, dy) in enumerate(BLOCKS):
        comes, _ = neighbour(counts, -sign * dx, -sign * dy)

        @pl.when(jnp.logical_not(comes))
        def _():
            view = target(k)
            view[...] = jnp.zeros(view.shape, view.dtype)


def edge_views(sz, sides, tiles):
    def view(k):
        if k < 4:
            return sides.at[pl.ds(*sz.sides[k])]
        return tiles.at[pl.ds((k - 4) * CORNER_ROWS, CORNER_ROWS)]

    return view


def kernel(sz, counts, capacity, base, offset, vel, aff, vol, mask, direction, out, *scratch):
    (
        tabs, right, depth_w, depth_s, result, inner_sums, edge_total, total, speed, keep, wide, wide_edge,
        ratio, chosen, slots, packed, xw, xs, yw, ys,
        margins, corners, got, got_corners, sent, sent_corners, halo, halo_corners, spread,
        buckets, arrived, send_sems, recv_sems, bucket_sends, bucket_recvs,
    ) = scratch
    size_x, size_y, depth = sz.x, sz.y, sz.depth
    width = sz.chunk
    tables = (xw, xs, yw, ys)
    greet(counts)

    margin_copies, halo_copies = ([], [])
    for s in range(2):
        arriving = edge_views(sz, got.at[s], got_corners.at[s])
        clear_missing(counts, 1, arriving)
        margin_copies.append(
            transfers(
                counts, 1, edge_views(sz, margins.at[s], corners.at[s]), arriving,
                send_sems.at[2 * s], recv_sems.at[2 * s],
            )
        )
        arriving = edge_views(sz, halo.at[s], halo_corners.at[s])
        clear_missing(counts, -1, arriving)
        halo_copies.append(
            transfers(
                counts, -1, edge_views(sz, sent.at[s], sent_corners.at[s]), arriving,
                send_sems.at[2 * s + 1], recv_sems.at[2 * s + 1],
            )
        )
    order = [0, 1, 2, 3, 5, 6, 7, 8]
    slot_of = [order.index(3 * (dx + 1) + dy + 1) for dx, dy in BLOCKS]
    clear_missing(counts, 1, lambda k: arrived.at[slot_of[k]])
    bucket_copies = transfers(
        counts, 1, lambda k: buckets.at[slot_of[k]], lambda k: arrived.at[slot_of[k]],
        bucket_sends, bucket_recvs,
    )
    for step in range(sz.steps):
        right[step, 0:depth, width : 3 * width] = jnp.zeros((depth, 2 * width), BF16)
        for s in range(2):
            tabs[s, step, sz.used : sz.edge] = jnp.zeros((sz.edge - sz.used, 3 * width), BF16)
    for y in range(size_y):
        column = mask[pl.ds(y, size_x, stride=size_y), :]
        keep[y * size_x : (y + 1) * size_x] = (1 - column).astype(F32)

    def lanes_of(step):
        return pl.ds(pl.multiple_of(step * width, width), width)

    def prepare(s, step):
        lanes = lanes_of(step)
        build(
            sz, base[:, s, lanes], offset[:, s, lanes], tabs.at[s, step], tables,
            depth_w.at[s, :, lanes], depth_s.at[s, :, lanes],
        )

    def scatter_edge(s, step):
        edge_total[...] += lax.dot_general(
            tabs[s, step, 0 : sz.used], right[step], NT, preferred_element_type=F32
        )

    def scatter_inner(s, step):
        added = lax.dot_general(
            tabs[s, step, sz.edge :], right[step], NT, preferred_element_type=F32
        )
        for c in range(4):
            total[c] += added[:, c * depth : (c + 1) * depth]

    def send_margins(s):
        margins[s] = edge_total[0 : sz.corner].astype(BF16)
        for k in range(4):
            for c in range(4):
                spread[k * 16 + 4 * c : k * 16 + 4 * c + 4, :] = edge_total[
                    sz.corner + 4 * k : sz.corner + 4 * k + 4, c * depth : (c + 1) * depth
                ]
        corners[s] = spread[...].astype(BF16)
        start_all(margin_copies[s])

    def add_margins(s):
        wait_arrivals(margin_copies[s])
        for k, low in ((1, 0), (0, sz.cells - 2 * size_x)):
            start, count = sz.sides[k]
            for c in range(4):
                block = got[s, start : start + count, c * depth : (c + 1) * depth]
                total[c, low : low + count] += block.astype(F32)
        for k, low in ((2, size_x - 2), (3, 0)):
            start = sz.sides[k][0]
            block = got[s, start : start + 2 * size_y].astype(F32)
            for i in range(2):
                rows = pl.ds(low + i, size_y, stride=size_x)
                for c in range(4):
                    lanes = slice(c * depth, (c + 1) * depth)
                    total[c, rows] += block[i * size_y : (i + 1) * size_y, lanes]
        spread[...] = got_corners[s].astype(F32)
        for k, (dx, dy) in enumerate(CORNERS):
            low_x = size_x - 2 if dx < 0 else 0
            low_y = size_y - 2 if dy < 0 else 0
            for i in range(2):
                for j in range(2):
                    row = (low_y + j) * size_x + low_x + i
                    for c in range(4):
                        here = k * 16 + 4 * c + 2 * i + j
                        total[c, row : row + 1] += spread[here : here + 1]

    def velocities():
        mass = jnp.maximum(total[0], MASS_FLOOR)
        for axis in range(3):
            value = total[axis + 1] / mass
            if axis == 2:
                value = value - TIME_STEP * GRAVITY
            speed[axis] = value * keep[...]

    def send_halo(s):
        for k, low in ((1, 0), (0, sz.cells - 2 * size_x)):
            start, count = sz.sides[k]
            for c in range(3):
                lanes = slice(c * depth, (c + 1) * depth)
                sent[s, start : start + count, lanes] = speed[c, low : low + count].astype(BF16)
        for k, low in ((2, size_x - 2), (3, 0)):
            for i in range(2):
                start = sz.sides[k][0] + i * size_y
                rows = pl.ds(low + i, size_y, stride=size_x)
                for c in range(3):
                    lanes = slice(c * depth, (c + 1) * depth)
                    sent[s, start : start + size_y, lanes] = speed[c, rows].astype(BF16)
        for k, (dx, dy) in enumerate(CORNERS):
            low_x = size_x - 2 if dx < 0 else 0
            low_y = size_y - 2 if dy < 0 else 0
            for i in range(2):
                for j in range(2):
                    row = (low_y + j) * size_x + low_x + i
                    for c in range(3):
                        here = k * 16 + 4 * c + 2 * i + j
                        spread[here : here + 1] = speed[c, row : row + 1]
        sent_corners[s] = spread[...].astype(BF16)
        start_all(halo_copies[s])

    def fill_wide():
        for c in range(3):
            wide[c * depth : (c + 1) * depth, :] = speed[c].T.astype(BF16)

    def fill_wide_edge(s):
        wait_arrivals(halo_copies[s])
        spread[...] = halo_corners[s].astype(F32)
        for c in range(3):
            lanes = slice(c * depth, (c + 1) * depth)
            tiles = [spread[k * 16 + 4 * c : k * 16 + 4 * c + 4] for k in range(4)]
            rest = jnp.zeros((sz.edge - sz.used, depth), F32)
            outer = jnp.concatenate([halo[s, :, lanes].astype(F32)] + tiles + [rest], 0)
            wide_edge[lanes, :] = outer.T.astype(BF16)

    def gather_inner(s, step):
        lanes = lanes_of(step)
        result[...] = jnp.dot(wide[...], tabs[s, step, sz.edge :], preferred_element_type=F32)
        sums = reduce_depth(sz, result, depth_w.at[s, :, lanes], depth_s.at[s, :, lanes])
        for k in range(12):
            inner_sums[k, :, lanes] = sums[k]

    def gather_edge(s, step, volume):
        lanes = lanes_of(step)
        result[...] = jnp.dot(wide_edge[...], tabs[s, step, 0 : sz.edge], preferred_element_type=F32)
        sums = reduce_depth(sz, result, depth_w.at[s, :, lanes], depth_s.at[s, :, lanes])
        return finish([sums[k] + inner_sums[k, :, lanes] for k in range(12)], volume)

    def loop(body):
        lax.fori_loop(0, sz.steps, lambda step, carry: (body(step), carry)[1], 0)

    def rows_of(ref, lanes, count):
        return [ref[k : k + 1, lanes] for k in range(count)]

    edge_total[...] = jnp.zeros_like(edge_total)
    total[...] = jnp.zeros_like(total)

    def first(step):
        lanes = lanes_of(step)
        prepare(0, step)
        build_right(
            sz, rows_of(vel, lanes, 3), rows_of(aff, lanes, 9), vol[:, lanes],
            depth_w.at[0, :, lanes], depth_s.at[0, :, lanes], right.at[step],
        )
        scatter_edge(0, step)

    def first_inner(step):
        scatter_inner(0, step)
        prepare(1, step)

    def second(step):
        lanes = lanes_of(step)
        new_vel, new_aff, new_vol = gather_edge(0, step, vol[:, lanes])
        ratio[:, lanes] = new_vol
        build_right(
            sz, new_vel, new_aff, new_vol, depth_w.at[1, :, lanes], depth_s.at[1, :, lanes],
            right.at[step],
        )
        scatter_edge(1, step)

    index_x = lax.axis_index("gx")
    index_y = lax.axis_index("gy")

    def route(code):
        step_x = jnp.where(code < 3, -1, jnp.where(code > 5, 1, 0))
        step_y = code - 3 * step_x - 4
        to_x = step_x + index_x
        to_y = step_y + index_y
        inside = (to_x >= 0) & (to_x < counts[0]) & (to_y >= 0) & (to_y < counts[1])
        return (
            jnp.where(inside, code, 4),
            jnp.where(inside, step_x, 0),
            jnp.where(inside, step_y, 0),
        )

    def rank_rows():
        parts = sz.rows // LANES
        place = rows_iota(8)
        codes = jnp.where(place < 4, place, place + 1)
        hits = []
        for part in range(parts):
            moving, _, _ = route(direction[:, part * LANES : (part + 1) * LANES])
            hits.append(jnp.where(moving == codes, 1.0, 0.0))
        above = lax.broadcasted_iota(jnp.int32, (LANES, 2 * LANES), 0)
        along = lax.broadcasted_iota(jnp.int32, (LANES, 2 * LANES), 1)
        summer = jnp.where(above <= along, 1.0, 0.0).astype(BF16)
        sums = jnp.dot(
            jnp.concatenate(hits, 0).astype(BF16), summer, preferred_element_type=F32
        )
        before = jnp.broadcast_to((place * capacity).astype(F32), (8, LANES))
        for part in range(parts):
            mine = slice(part * 8, (part + 1) * 8)
            slot = jnp.sum(hits[part] * (sums[mine, 0:LANES] + before), 0, keepdims=True) - 1.0
            slots[:, part * LANES : (part + 1) * LANES] = slot.astype(jnp.int32)
            before = before + sums[mine, LANES:]

    def second_inner(step):
        lanes = lanes_of(step)
        scatter_inner(1, step)
        slot = slots[:, lanes]
        for k in range(8):
            here = slot - k * capacity == rows_iota(capacity)
            chosen[k * capacity : (k + 1) * capacity, lanes] = jnp.where(here, 1.0, 0.0).astype(BF16)

    def last(step):
        lanes = lanes_of(step)
        new_vel, new_aff, new_vol = gather_edge(1, step, ratio[:, lanes])
        moving, step_x, step_y = route(direction[:, lanes])
        shift = (step_x * size_x, step_y * size_y, None)
        bases = base[:, 1, lanes]
        offsets = offset[:, 1, lanes]
        spots = []
        for axis in range(3):
            spot = bases[axis : axis + 1].astype(F32) + offsets[axis : axis + 1]
            spot = spot + TIME_STEP * new_vel[axis]
            if shift[axis] is not None:
                spot = spot - shift[axis].astype(F32)
            spots.append(spot)
        value = jnp.concatenate(spots + new_vel + new_aff + [new_vol], 0)
        out[:, lanes] = jnp.where(moving == 4, value, 0.0)
        high = value.astype(BF16)
        rest = value - high.astype(F32)
        middle = rest.astype(BF16)
        low = (rest - middle.astype(F32)).astype(BF16)
        parts = jnp.concatenate([high, middle, low], 0)
        packed[...] += lax.dot_general(parts, chosen[:, lanes], NT, preferred_element_type=F32)

    loop(first)
    await_peers(counts)
    send_margins(0)
    loop(first_inner)
    add_margins(0)
    velocities()
    send_halo(0)
    fill_wide()
    loop(lambda step: gather_inner(0, step))
    rank_rows()
    fill_wide_edge(0)
    edge_total[...] = jnp.zeros_like(edge_total)
    total[...] = jnp.zeros_like(total)
    loop(second)
    send_margins(1)
    loop(second_inner)
    add_margins(1)
    velocities()
    send_halo(1)
    fill_wide()
    loop(lambda step: gather_inner(1, step))
    packed[...] = jnp.zeros_like(packed)
    fill_wide_edge(1)
    loop(last)
    for k in range(8):
        lanes = slice(k * capacity, (k + 1) * capacity)
        buckets[k] = packed[0:16, lanes] + packed[16:32, lanes] + packed[32:48, lanes]
    start_all(bucket_copies)
    wait_arrivals(bucket_copies)
    for k in range(8):
        out[:, sz.rows + k * capacity : sz.rows + (k + 1) * capacity] = arrived[k]
    for copies in margin_copies + halo_copies + [bucket_copies]:
        wait_sends(copies)


def vmem(count):
    return [pl.BlockSpec(memory_space=pltpu.VMEM)] * count


def per_device(counts, base, offset, velocity, affine, volume, node_mask, direction):
    size_x, size_y, depth = node_mask.shape
    rows = velocity.shape[1]
    capacity = rows // 16
    sz = Sizes(size_x, size_y, depth, rows, min(rows, 512))
    base = jnp.swapaxes(base, 0, 1)
    offset = jnp.swapaxes(offset, 0, 1)
    volume = volume.reshape(1, rows)
    direction = direction.reshape(1, rows)
    mask = node_mask.reshape(sz.cells, depth)
    width = sz.chunk
    scratch = [
        pltpu.VMEM((2, sz.steps, sz.edge + sz.cells, 3 * width), BF16),
        pltpu.VMEM((sz.steps, 4 * depth, 3 * width), BF16),
        pltpu.VMEM((2, depth, rows), F32),
        pltpu.VMEM((2, depth, rows), F32),
        pltpu.VMEM((3 * depth, 3 * width), F32),
        pltpu.VMEM((12, 8, rows), F32),
        pltpu.VMEM((sz.used, 4 * depth), F32),
        pltpu.VMEM((4, sz.cells, depth), F32),
        pltpu.VMEM((3, sz.cells, depth), F32),
        pltpu.VMEM((sz.cells, depth), F32),
        pltpu.VMEM((3 * depth, sz.cells), BF16),
        pltpu.VMEM((3 * depth, sz.edge), BF16),
        pltpu.VMEM((1, rows), F32),
        pltpu.VMEM((8 * capacity, rows), BF16),
        pltpu.VMEM((1, rows), jnp.int32),
        pltpu.VMEM((48, 8 * capacity), F32),
        pltpu.VMEM((size_x + 8, width), F32),
        pltpu.VMEM((size_x + 8, width), F32),
        pltpu.VMEM((size_y + 8, width), F32),
        pltpu.VMEM((size_y + 8, width), F32),
    ]
    for lanes in (4 * depth, 4 * depth, 3 * depth, 3 * depth):
        scratch.append(pltpu.VMEM((2, sz.corner, lanes), BF16))
        scratch.append(pltpu.VMEM((2, 4 * CORNER_ROWS, depth), BF16))
    scratch += [
        pltpu.VMEM((4 * CORNER_ROWS, depth), F32),
        pltpu.VMEM((8, 16, capacity), F32),
        pltpu.VMEM((8, 16, capacity), F32),
        pltpu.SemaphoreType.DMA((4, 8)),
        pltpu.SemaphoreType.DMA((4, 8)),
        pltpu.SemaphoreType.DMA((8,)),
        pltpu.SemaphoreType.DMA((8,)),
    ]
    return pl.pallas_call(
        functools.partial(kernel, sz, counts, capacity),
        out_shape=jax.ShapeDtypeStruct((16, rows + 8 * capacity), F32),
        in_specs=vmem(7),
        out_specs=vmem(1)[0],
        scratch_shapes=scratch,
        compiler_params=pltpu.CompilerParams(
            collective_id=0, has_side_effects=True, vmem_limit_bytes=60 * 1024 * 1024
        ),
        name="substeps",
    )(base, offset, velocity, affine, volume, mask, direction)


def solution(mesh):
    counts = (mesh.shape["gx"], mesh.shape["gy"])
    placed = (
        P(None, None, ("gx", "gy")),
        P(None, None, ("gx", "gy")),
        P(None, ("gx", "gy")),
        P(None, ("gx", "gy")),
        P(("gx", "gy")),
        P("gx", "gy", None),
        P(("gx", "gy")),
    )
    return jax.shard_map(
        functools.partial(per_device, counts),
        mesh=mesh,
        in_specs=placed,
        out_specs=P(None, ("gx", "gy")),
        check_vma=False,
    )
```

time: 52.5 us -> 40.8 us (0.78)
  Pallas kernels: 50.7 us -> 38.9 us
    pallas_call x3 -> x1, Pallas kernels: 50.7 us -> 38.9 us  [per_device(): pl.pallas_call(functools.partial(kernel, sz, counts, capacity), out_shape...]
where the time goes in v1:
time: 40.8 us; the launch traced here: 40.5 us
  Pallas kernels  38.9 us (95%)
  local copies, waits for them, and re-layouts  1.62 us (4%)
    pallas_call x1, Pallas kernels, per_device(): pl.pallas_call(functools.partial(kernel, sz, counts, capacity), out_shape...  38.9 us
    unnamed x1, local copies, waits for them, and re-layouts  1.62 us

profile of v1, /device:TPU:0, one launch (start us, length us, event | category | flops | bytes accessed | tf_op | source)
XLA Modules:
  0.0 40.5 jit_solution(9046815854641113910)
XLA Ops:
  0.0 38.9 %substeps.1 = f32[16,3072]{1,0:T(8,128)} custom-call(s32[3,2,2048]{2,1,0:T(2,128)} %bitcast.6, f32[3,2,2048]{2,1,0:T(2,128)} %bitcast.7, f32[3,2048]{1,0:T(4,128)} %vel.1, f32[9,2048]{1,0:T(8,128)} %aff.1, f32[1,2048]{1,0:T(1,128)} %bitcast.8, s32[512,128]{1,0:T(8,128)} %bitcast.5, s32[1,2048]{1,0:T(1,128)} %bitcast.9), custom_call_target="tpu_custom_call" | custom-call | tf_op jit(solution)/shard_map/substeps/pallas_call | solution.py:586
  38.9 1.6 %copy.9 = f32[16,3072]{1,0:T(8,128)} copy(f32[16,3072]{1,0:T(8,128)} %substeps.1) | data formatting | bytes 393216

commit v2 on v1

v2 whole, which is shorter than its diff:
```python
import functools

import jax
import jax.numpy as jnp
from jax import lax
from jax.experimental import pallas as pl
from jax.experimental.pallas import tpu as pltpu
from jax.sharding import PartitionSpec as P

PARTICLE_MASS = 1.0
STIFFNESS = 4.0
TIME_STEP = 0.1
GRAVITY = 3.0
MASS_FLOOR = 0.5
LANES = 128
OUTSIDE = -100

F32 = jnp.float32
BF16 = jnp.bfloat16
NT = (((1,), (1,)), ((), ()))

SIDES = ((0, -1), (0, 1), (-1, 0), (1, 0))
CORNERS = ((-1, -1), (-1, 1), (1, -1), (1, 1))
BLOCKS = SIDES + CORNERS
ISSUE = (4, 5, 6, 7, 0, 1, 2, 3)
CORNER_ROWS = 16
UNROLL = (False,) * 7


class Sizes:
    def __init__(self, size_x, size_y, depth, rows, chunk):
        self.x, self.y, self.depth, self.rows, self.chunk = size_x, size_y, depth, rows, chunk
        self.steps = rows // chunk
        self.cells = size_x * size_y
        counts = [2 * size_x] * 2 + [2 * size_y] * 2
        self.sides = [(sum(counts[:k]), counts[k]) for k in range(4)]
        self.corner = sum(counts)
        self.used = self.corner + 16
        self.edge = self.used


def spline(frac):
    return [0.5 * (1.5 - frac) ** 2, 0.75 - (frac - 1.0) ** 2, 0.5 * (frac - 0.5) ** 2]


def pick(place, values):
    return jnp.where(
        place == 0,
        values[0],
        jnp.where(place == 1, values[1], jnp.where(place == 2, values[2], 0.0)),
    )


def weights_of(offsets):
    weights = spline(offsets)
    return (weights, [weights[node] * (float(node) - offsets) for node in range(3)])


def rows_iota(count):
    return lax.broadcasted_iota(jnp.int32, (count, 1), 0)


def groups(width):
    return [slice(low, low + LANES) for low in range(0, width, LANES)]


def put(tab, width, group, row, count, wx, sx, wy, sy):
    for third, value in enumerate((wx * wy, sx * wy, wx * sy)):
        low = third * width + group.start
        tab[row : row + count, low : low + LANES] = value.astype(BF16)


def build_edge(sz, bases, offsets, tab, tables):
    all_weights, all_slopes = weights_of(offsets)
    edge = rows_iota(8)
    for group in groups(sz.chunk):
        weights = [[value[axis : axis + 1, group] for value in all_weights] for axis in range(3)]
        slopes = [[value[axis : axis + 1, group] for value in all_slopes] for axis in range(3)]
        from_x = bases[0:1, group] + 2
        from_y = bases[1:2, group] + 2
        pairs = []
        for size, start, axis in ((sz.x, from_x, 0), (sz.y, from_y, 1)):
            place = rows_iota(size) + 2 - start
            plain, slope = (pick(place, weights[axis]), pick(place, slopes[axis]))
            tables[2 * axis][0:size, group] = plain
            tables[2 * axis + 1][0:size, group] = slope
            place = jnp.where(edge < 2, edge, jnp.where(edge < 4, edge + size, OUTSIDE)) - start
            pairs.append((plain, slope, pick(place, weights[axis]), pick(place, slopes[axis])))
        wide_w, wide_s, out_xw, out_xs = pairs[0]
        tall_w, tall_s, out_yw, out_ys = pairs[1]
        for k in range(4):
            one = slice(k, k + 1)
            put(tab, sz.chunk, group, k * sz.x, sz.x, wide_w, wide_s, out_yw[one], out_ys[one])
        for k in range(4):
            one = slice(k, k + 1)
            row = sz.sides[2][0] + k * sz.y
            put(tab, sz.chunk, group, row, sz.y, out_xw[one], out_xs[one], tall_w, tall_s)
        spot = rows_iota(16)
        place_x = ((spot >> 1) & 1) + (spot >> 3) * (sz.x + 2) - from_x
        place_y = (spot & 1) + ((spot >> 2) & 1) * (sz.y + 2) - from_y
        put(
            tab, sz.chunk, group, sz.corner, 16, pick(place_x, weights[0]), pick(place_x, slopes[0]),
            pick(place_y, weights[1]), pick(place_y, slopes[1]),
        )


def build_depth(sz, bases, offsets, depth_w, depth_s):
    all_weights, all_slopes = weights_of(offsets[2:3])
    for group in groups(sz.chunk):
        place = rows_iota(sz.depth) - bases[2:3, group]
        depth_w[:, group] = pick(place, [value[:, group] for value in all_weights])
        depth_s[:, group] = pick(place, [value[:, group] for value in all_slopes])


def build_inner(sz, tab, tables):
    xw, xs, yw, ys = tables
    for group in groups(sz.chunk):
        wide_w, wide_s = (xw[0 : sz.x, group], xs[0 : sz.x, group])
        for y in range(sz.y):
            one = slice(y, y + 1)
            put(
                tab, sz.chunk, group, sz.edge + y * sz.x, sz.x, wide_w, wide_s,
                yw[one, group], ys[one, group],
            )


def build_right(sz, vel, aff, vol, depth_w, depth_s, right):
    depth = sz.depth
    width = sz.chunk
    all_stress = -STIFFNESS * (vol - 1.0)
    for group in groups(width):
        stress = all_stress[:, group]

        def entry(i, j):
            value = PARTICLE_MASS * aff[3 * i + j][:, group]
            return value + stress if i == j else value

        def store(third, rows, value):
            low = third * width + group.start
            right[rows, low : low + LANES] = value.astype(BF16)

        plain = depth_w[:, group]
        slope = depth_s[:, group]
        store(0, slice(0, depth), plain * PARTICLE_MASS)
        for i in range(3):
            rows = slice((i + 1) * depth, (i + 2) * depth)
            moment = PARTICLE_MASS * vel[i][:, group]
            store(0, rows, plain * moment + slope * entry(i, 2))
            store(1, rows, plain * entry(i, 0))
            store(2, rows, plain * entry(i, 1))


def reduce_depth(sz, result, depth_w, depth_s):
    parts = []

    def fold(value):
        return jnp.sum(value.reshape(sz.depth // 8, 8, LANES), 0)

    for group in groups(sz.chunk):
        weight, slope = (depth_w[:, group], depth_s[:, group])
        sums = []
        for i in range(3):
            rows = slice(i * sz.depth, (i + 1) * sz.depth)
            thirds = [
                result[rows, third * sz.chunk + group.start : third * sz.chunk + group.stop]
                for third in range(3)
            ]
            sums += [fold(third * weight) for third in thirds] + [fold(thirds[0] * slope)]
        parts.append(sums)
    return [jnp.concatenate([sums[k] for sums in parts], 1) for k in range(12)]


def finish(sums, vol):
    vel = [jnp.sum(sums[4 * i], 0, keepdims=True) for i in range(3)]
    aff = [
        4.0 * jnp.sum(sums[4 * i + 1 + a], 0, keepdims=True) for i in range(3) for a in range(3)
    ]
    return (vel, aff, vol * (1.0 + TIME_STEP * (aff[0] + aff[4] + aff[8])))


def neighbour(counts, dx, dy):
    to_x = lax.axis_index("gx") + dx
    to_y = lax.axis_index("gy") + dy
    exists = (to_x >= 0) & (to_x < counts[0]) & (to_y >= 0) & (to_y < counts[1])
    return (exists, {"gx": to_x, "gy": to_y})


def greet(counts):
    barrier = pltpu.get_barrier_semaphore()
    for dx, dy in BLOCKS:
        exists, where = neighbour(counts, dx, dy)

        @pl.when(exists)
        def _():
            pl.semaphore_signal(
                barrier, inc=1, device_id=where, device_id_type=pl.DeviceIdType.MESH
            )


def await_peers(counts):
    barrier = pltpu.get_barrier_semaphore()
    peers = 0
    for dx, dy in BLOCKS:
        exists, _ = neighbour(counts, dx, dy)
        peers = peers + exists.astype(jnp.int32)
    pl.semaphore_wait(barrier, peers)


def transfers(counts, sign, source, target, send_sems, recv_sems):
    copies = []
    for k, (dx, dy) in enumerate(BLOCKS):
        exists, where = neighbour(counts, sign * dx, sign * dy)
        copy = pltpu.make_async_remote_copy(
            src_ref=source(k),
            dst_ref=target(k),
            send_sem=send_sems.at[k],
            recv_sem=recv_sems.at[k],
            device_id=where,
            device_id_type=pl.DeviceIdType.MESH,
        )
        comes, _ = neighbour(counts, -sign * dx, -sign * dy)
        copies.append((exists, comes, copy))
    return copies


def start_all(copies, picked=ISSUE):
    for k in picked:
        pl.when(copies[k][0])(copies[k][2].start)


def wait_arrivals(copies, picked=ISSUE):
    for k in picked:
        pl.when(copies[k][1])(copies[k][2].wait_recv)


def wait_sends(copies):
    for exists, _, copy in copies:
        pl.when(exists)(copy.wait_send)


def clear_missing(counts, sign, target):
    for k, (dx, dy) in enumerate(BLOCKS):
        comes, _ = neighbour(counts, -sign * dx, -sign * dy)

        @pl.when(jnp.logical_not(comes))
        def _():
            view = target(k)
            view[...] = jnp.zeros(view.shape, view.dtype)


def edge_views(sz, sides, tiles):
    def view(k):
        if k < 4:
            return sides.at[pl.ds(*sz.sides[k])]
        return tiles.at[pl.ds((k - 4) * CORNER_ROWS, CORNER_ROWS)]

    return view


def kernel(sz, counts, capacity, *refs):
    held, placed, out, scratch = (refs[:7], refs[7], refs[15], refs[16:])
    base, offset, vel, aff, vol, mask, direction = refs[8:15]
    loads = [
        pltpu.make_async_copy(held[k], refs[8 + k], scratch[-1].at[k]) for k in range(7)
    ]
    for load in loads:
        load.start()
    (
        tabs, right, depth_w, depth_s, result, inner_sums, edge_total, total, speed, keep, wide, wide_edge,
        ratio, chosen, hits, masked, packed, xw, xs, yw, ys,
        margins, corners, got, got_corners, sent, sent_corners, halo, halo_corners, spread,
        buckets, nothing, send_sems, recv_sems, bucket_sends, bucket_recvs,
    ) = scratch[:-1]
    size_x, size_y, depth = sz.x, sz.y, sz.depth
    width = sz.chunk
    greet(counts)

    margin_copies, halo_copies = ([], [])
    for s in range(2):
        arriving = edge_views(sz, got.at[s], got_corners.at[s])
        margin_copies.append(
            transfers(
                counts, 1, edge_views(sz, margins.at[s], corners.at[s]), arriving,
                send_sems.at[2 * s], recv_sems.at[2 * s],
            )
        )
        arriving = edge_views(sz, halo.at[s], halo_corners.at[s])
        halo_copies.append(
            transfers(
                counts, -1, edge_views(sz, sent.at[s], sent_corners.at[s]), arriving,
                send_sems.at[2 * s + 1], recv_sems.at[2 * s + 1],
            )
        )
    order = [0, 1, 2, 3, 5, 6, 7, 8]
    slot_of = [order.index(3 * (dx + 1) + dy + 1) for dx, dy in BLOCKS]

    def bucket_place(k):
        return placed.at[:, pl.ds(sz.rows + slot_of[k] * capacity, capacity)]

    bucket_copies = transfers(
        counts, 1, lambda k: buckets.at[slot_of[k]], bucket_place, bucket_sends, bucket_recvs
    )
    clears = []
    for k in range(8):
        clear_copy = pltpu.make_async_copy(nothing, bucket_place(k), scratch[-1].at[8 + k])
        clears.append((jnp.logical_not(bucket_copies[k][1]), clear_copy))
    def lanes_of(step):
        if isinstance(step, int):
            return slice(step * width, (step + 1) * width)
        return pl.ds(pl.multiple_of(step * width, width), width)

    def clear():
        for s in range(2):
            clear_missing(counts, 1, edge_views(sz, got.at[s], got_corners.at[s]))
            clear_missing(counts, -1, edge_views(sz, halo.at[s], halo_corners.at[s]))
        nothing[...] = jnp.zeros_like(nothing)
        for missing, clear_copy in clears:
            pl.when(missing)(clear_copy.start)
        loads[5].wait()
        for y in range(size_y):
            column = mask[pl.ds(y, size_x, stride=size_y), :]
            keep[y * size_x : (y + 1) * size_x] = (1 - column).astype(F32)

    def tables_of(step):
        return [table.at[step] for table in (xw, xs, yw, ys)]

    def prepare(s, step):
        lanes = lanes_of(step)
        build_edge(sz, base[:, s, lanes], offset[:, s, lanes], tabs.at[s, step], tables_of(step))

    def prepare_depth(s, step):
        lanes = lanes_of(step)
        build_depth(
            sz, base[:, s, lanes], offset[:, s, lanes],
            depth_w.at[s, :, lanes], depth_s.at[s, :, lanes],
        )

    def scatter_edge(s, step):
        edge_total[...] += lax.dot_general(
            tabs[s, step, 0 : sz.used], right[step], NT, preferred_element_type=F32
        )

    def scatter_inner(s, step):
        added = lax.dot_general(
            tabs[s, step, sz.edge :], right[step], NT, preferred_element_type=F32
        )
        for c in range(4):
            total[c] += added[:, c * depth : (c + 1) * depth]

    def send_margins(s):
        margins[s] = edge_total[0 : sz.corner].astype(BF16)
        for k in range(4):
            for c in range(4):
                spread[k * 16 + 4 * c : k * 16 + 4 * c + 4, :] = edge_total[
                    sz.corner + 4 * k : sz.corner + 4 * k + 4, c * depth : (c + 1) * depth
                ]
        corners[s] = spread[...].astype(BF16)
        start_all(margin_copies[s])

    def add_margins(s):
        wait_arrivals(margin_copies[s])
        for k, low in ((1, 0), (0, sz.cells - 2 * size_x)):
            start, count = sz.sides[k]
            for c in range(4):
                block = got[s, start : start + count, c * depth : (c + 1) * depth]
                total[c, low : low + count] += block.astype(F32)
        for k, low in ((2, size_x - 2), (3, 0)):
            start = sz.sides[k][0]
            block = got[s, start : start + 2 * size_y].astype(F32)
            for i in range(2):
                rows = pl.ds(low + i, size_y, stride=size_x)
                for c in range(4):
                    lanes = slice(c * depth, (c + 1) * depth)
                    total[c, rows] += block[i * size_y : (i + 1) * size_y, lanes]
        spread[...] = got_corners[s].astype(F32)
        for k, (dx, dy) in enumerate(CORNERS):
            low_x = size_x - 2 if dx < 0 else 0
            low_y = size_y - 2 if dy < 0 else 0
            for i in range(2):
                for j in range(2):
                    row = (low_y + j) * size_x + low_x + i
                    for c in range(4):
                        here = k * 16 + 4 * c + 2 * i + j
                        total[c, row : row + 1] += spread[here : here + 1]

    def velocities(low, count):
        rows = slice(low, low + count)
        mass = jnp.maximum(total[0, rows], MASS_FLOOR)
        for axis in range(3):
            value = total[axis + 1, rows] / mass
            if axis == 2:
                value = value - TIME_STEP * GRAVITY
            speed[axis, rows] = value * keep[rows]

    def send_halo(s):
        border = 2 * size_x
        for k, low in ((1, 0), (0, sz.cells - border)):
            velocities(low, border)
            start, count = sz.sides[k]
            for c in range(3):
                lanes = slice(c * depth, (c + 1) * depth)
                sent[s, start : start + count, lanes] = speed[c, low : low + count].astype(BF16)
        for k, (dx, dy) in enumerate(CORNERS):
            low_x = size_x - 2 if dx < 0 else 0
            low_y = size_y - 2 if dy < 0 else 0
            for i in range(2):
                for j in range(2):
                    row = (low_y + j) * size_x + low_x + i
                    for c in range(3):
                        here = k * 16 + 4 * c + 2 * i + j
                        spread[here : here + 1] = speed[c, row : row + 1]
        sent_corners[s] = spread[...].astype(BF16)
        start_all(halo_copies[s], ISSUE[:6])
        velocities(border, sz.cells - 2 * border)
        for k, low in ((2, size_x - 2), (3, 0)):
            for i in range(2):
                start = sz.sides[k][0] + i * size_y
                rows = pl.ds(low + i, size_y, stride=size_x)
                for c in range(3):
                    lanes = slice(c * depth, (c + 1) * depth)
                    sent[s, start : start + size_y, lanes] = speed[c, rows].astype(BF16)
        start_all(halo_copies[s], ISSUE[6:])

    def fill_wide():
        for c in range(3):
            wide[c * depth : (c + 1) * depth, :] = speed[c].T.astype(BF16)

    def fill_wide_edge(s):
        wait_arrivals(halo_copies[s])
        spread[...] = halo_corners[s].astype(F32)
        for c in range(3):
            lanes = slice(c * depth, (c + 1) * depth)
            tiles = [spread[k * 16 + 4 * c : k * 16 + 4 * c + 4] for k in range(4)]
            outer = jnp.concatenate([halo[s, :, lanes].astype(F32)] + tiles, 0)
            wide_edge[lanes, :] = outer.T.astype(BF16)

    def gather_inner(s, step):
        lanes = lanes_of(step)
        here = result.at[step % 2]
        here[...] = jnp.dot(wide[...], tabs[s, step, sz.edge :], preferred_element_type=F32)
        sums = reduce_depth(sz, here, depth_w.at[s, :, lanes], depth_s.at[s, :, lanes])
        for k in range(12):
            inner_sums[k, :, lanes] = sums[k]

    def gather_edge(s, step, volume):
        lanes = lanes_of(step)
        here = result.at[step % 2]
        here[...] = jnp.dot(wide_edge[...], tabs[s, step, 0 : sz.edge], preferred_element_type=F32)
        sums = reduce_depth(sz, here, depth_w.at[s, :, lanes], depth_s.at[s, :, lanes])
        return finish([sums[k] + inner_sums[k, :, lanes] for k in range(12)], volume)

    def loop(body, unrolled):
        if unrolled:
            for step in range(sz.steps):
                body(step)
        else:
            lax.fori_loop(0, sz.steps, lambda step, carry: (body(step), carry)[1], 0)

    def rows_of(ref, lanes, count):
        return [ref[k : k + 1, lanes] for k in range(count)]

    def first(step):
        lanes = lanes_of(step)
        right[step, 0:depth, width : 3 * width] = jnp.zeros((depth, 2 * width), BF16)
        prepare(0, step)
        prepare_depth(0, step)
        build_right(
            sz, rows_of(vel, lanes, 3), rows_of(aff, lanes, 9), vol[:, lanes],
            depth_w.at[0, :, lanes], depth_s.at[0, :, lanes], right.at[step],
        )
        scatter_edge(0, step)

    def first_inner(step):
        build_inner(sz, tabs.at[0, step], tables_of(step))
        scatter_inner(0, step)
        prepare_depth(1, step)

    def first_gather(step):
        gather_inner(0, step)
        prepare(1, step)

    def second(step):
        lanes = lanes_of(step)
        new_vel, new_aff, new_vol = gather_edge(0, step, vol[:, lanes])
        ratio[:, lanes] = new_vol
        build_right(
            sz, new_vel, new_aff, new_vol, depth_w.at[1, :, lanes], depth_s.at[1, :, lanes],
            right.at[step],
        )
        scatter_edge(1, step)

    index_x = lax.axis_index("gx")
    index_y = lax.axis_index("gy")

    def route(code):
        step_x = jnp.where(code < 3, -1, jnp.where(code > 5, 1, 0))
        step_y = code - 3 * step_x - 4
        to_x = step_x + index_x
        to_y = step_y + index_y
        inside = (to_x >= 0) & (to_x < counts[0]) & (to_y >= 0) & (to_y < counts[1])
        return (
            jnp.where(inside, code, 4),
            jnp.where(inside, step_x, 0),
            jnp.where(inside, step_y, 0),
        )

    def rank_rows():
        parts = sz.rows // LANES
        place = rows_iota(8)
        codes = jnp.where(place < 4, place, place + 1)
        marks = []
        for part in range(parts):
            moving, _, _ = route(direction[:, part * LANES : (part + 1) * LANES])
            marks.append(jnp.where(moving == codes, 1.0, 0.0))
        above = lax.broadcasted_iota(jnp.int32, (LANES, 2 * LANES), 0)
        along = lax.broadcasted_iota(jnp.int32, (LANES, 2 * LANES), 1)
        summer = jnp.where(above <= along, 1.0, 0.0).astype(BF16)
        sums = jnp.dot(
            jnp.concatenate(marks, 0).astype(BF16), summer, preferred_element_type=F32
        )
        before = jnp.zeros((8, LANES), F32)
        for part in range(parts):
            mine = slice(part * 8, (part + 1) * 8)
            lanes = slice(part * LANES, (part + 1) * LANES)
            rank = jnp.sum(marks[part] * (sums[mine, 0:LANES] + before), 0, keepdims=True) - 1.0
            here = rank.astype(jnp.int32) == rows_iota(capacity)
            chosen[:, lanes] = jnp.where(here, 1.0, 0.0).astype(BF16)
            hits[:, lanes] = marks[part]
            before = before + sums[mine, LANES:]

    def second_inner(step):
        build_inner(sz, tabs.at[1, step], tables_of(step))
        scatter_inner(1, step)

    def last(step):
        lanes = lanes_of(step)
        new_vel, new_aff, new_vol = gather_edge(1, step, ratio[:, lanes])
        moving, step_x, step_y = route(direction[:, lanes])
        shift = (step_x * size_x, step_y * size_y, None)
        bases = base[:, 1, lanes]
        offsets = offset[:, 1, lanes]
        spots = []
        for axis in range(3):
            spot = bases[axis : axis + 1].astype(F32) + offsets[axis : axis + 1]
            spot = spot + TIME_STEP * new_vel[axis]
            if shift[axis] is not None:
                spot = spot - shift[axis].astype(F32)
            spots.append(spot)
        value = jnp.concatenate(spots + new_vel + new_aff + [new_vol], 0)
        out[:, lanes] = jnp.where(moving == 4, value, 0.0)
        high = value.astype(BF16).astype(F32)
        rest = value - high
        middle = rest.astype(BF16).astype(F32)
        for part, piece in enumerate((high, middle, rest - middle)):
            for k in range(8):
                row = (3 * k + part) * 16
                masked[step % 2, row : row + 16] = (piece * hits[k : k + 1, lanes]).astype(BF16)
        packed[...] += lax.dot_general(
            masked[step % 2], chosen[:, lanes], NT, preferred_element_type=F32
        )

    edge_total[...] = jnp.zeros_like(edge_total)
    for load in loads[:5]:
        load.wait()
    loop(first, UNROLL[0])
    await_peers(counts)
    send_margins(0)
    clear()
    total[...] = jnp.zeros_like(total)
    loop(first_inner, UNROLL[1])
    add_margins(0)
    send_halo(0)
    fill_wide()
    loop(first_gather, UNROLL[2])
    loads[6].wait()
    rank_rows()
    edge_total[...] = jnp.zeros_like(edge_total)
    fill_wide_edge(0)
    loop(second, UNROLL[3])
    send_margins(1)
    total[...] = jnp.zeros_like(total)
    loop(second_inner, UNROLL[4])
    add_margins(1)
    send_halo(1)
    fill_wide()
    loop(lambda step: gather_inner(1, step), UNROLL[5])
    packed[...] = jnp.zeros_like(packed)
    fill_wide_edge(1)
    loop(last, UNROLL[6])
    for k in range(8):
        rows = [slice((3 * k + part) * 16, (3 * k + part + 1) * 16) for part in range(3)]
        buckets[k] = packed[rows[0]] + packed[rows[1]] + packed[rows[2]]
    start_all(bucket_copies)
    store = pltpu.make_async_copy(out, placed.at[:, pl.ds(0, sz.rows)], scratch[-1].at[7])
    store.start()
    wait_arrivals(bucket_copies)
    for copies in margin_copies + halo_copies + [bucket_copies]:
        wait_sends(copies)
    for missing, clear_copy in clears:
        pl.when(missing)(clear_copy.wait)
    store.wait()


def per_device(counts, base, offset, velocity, affine, volume, node_mask, direction):
    size_x, size_y, depth = node_mask.shape
    rows = velocity.shape[1]
    capacity = rows // 16
    sz = Sizes(size_x, size_y, depth, rows, min(rows, 1024))
    base = jnp.swapaxes(base, 0, 1)
    offset = jnp.swapaxes(offset, 0, 1)
    volume = volume.reshape(1, rows)
    direction = direction.reshape(1, rows)
    mask = node_mask.reshape(sz.cells, depth)
    width = sz.chunk
    scratch = [pltpu.VMEM(x.shape, x.dtype) for x in (base, offset, velocity, affine, volume, mask, direction)]
    scratch += [
        pltpu.VMEM((16, rows), F32),
        pltpu.VMEM((2, sz.steps, sz.edge + sz.cells, 3 * width), BF16),
        pltpu.VMEM((sz.steps, 4 * depth, 3 * width), BF16),
        pltpu.VMEM((2, depth, rows), F32),
        pltpu.VMEM((2, depth, rows), F32),
        pltpu.VMEM((2, 3 * depth, 3 * width), F32),
        pltpu.VMEM((12, 8, rows), F32),
        pltpu.VMEM((sz.used, 4 * depth), F32),
        pltpu.VMEM((4, sz.cells, depth), F32),
        pltpu.VMEM((3, sz.cells, depth), F32),
        pltpu.VMEM((sz.cells, depth), F32),
        pltpu.VMEM((3 * depth, sz.cells), BF16),
        pltpu.VMEM((3 * depth, sz.edge), BF16),
        pltpu.VMEM((1, rows), F32),
        pltpu.VMEM((capacity, rows), BF16),
        pltpu.VMEM((8, rows), F32),
        pltpu.VMEM((2, 8 * 48, width), BF16),
        pltpu.VMEM((8 * 48, capacity), F32),
        pltpu.VMEM((sz.steps, size_x, width), F32),
        pltpu.VMEM((sz.steps, size_x, width), F32),
        pltpu.VMEM((sz.steps, size_y, width), F32),
        pltpu.VMEM((sz.steps, size_y, width), F32),
    ]
    for lanes in (4 * depth, 4 * depth, 3 * depth, 3 * depth):
        scratch.append(pltpu.VMEM((2, sz.corner, lanes), BF16))
        scratch.append(pltpu.VMEM((2, 4 * CORNER_ROWS, depth), BF16))
    scratch += [
        pltpu.VMEM((4 * CORNER_ROWS, depth), F32),
        pltpu.VMEM((8, 16, capacity), F32),
        pltpu.VMEM((16, capacity), F32),
        pltpu.SemaphoreType.DMA((4, 8)),
        pltpu.SemaphoreType.DMA((4, 8)),
        pltpu.SemaphoreType.DMA((8,)),
        pltpu.SemaphoreType.DMA((8,)),
        pltpu.SemaphoreType.DMA((16,)),
    ]
    return pl.pallas_call(
        functools.partial(kernel, sz, counts, capacity),
        out_shape=jax.ShapeDtypeStruct((16, rows + 8 * capacity), F32),
        in_specs=[pl.BlockSpec(memory_space=pltpu.HBM)] * 7,
        out_specs=pl.BlockSpec(memory_space=pltpu.HBM),
        scratch_shapes=scratch,
        compiler_params=pltpu.CompilerParams(
            collective_id=0, has_side_effects=True, vmem_limit_bytes=60 * 1024 * 1024
        ),
        name="substeps",
    )(base, offset, velocity, affine, volume, mask, direction)


def solution(mesh):
    counts = (mesh.shape["gx"], mesh.shape["gy"])
    placed = (
        P(None, None, ("gx", "gy")),
        P(None, None, ("gx", "gy")),
        P(None, ("gx", "gy")),
        P(None, ("gx", "gy")),
        P(("gx", "gy")),
        P("gx", "gy", None),
        P(("gx", "gy")),
    )
    return jax.shard_map(
        functools.partial(per_device, counts),
        mesh=mesh,
        in_specs=placed,
        out_specs=P(None, ("gx", "gy")),
        check_vma=False,
    )
```

time: 40.8 us -> 37.8 us (0.926)
  Pallas kernels: 38.9 us -> 36 us
    pallas_call x1, Pallas kernels: 38.9 us -> 36 us  [per_device(): pl.pallas_call(functools.partial(kernel, sz, counts, capacity), out_shape...]
where the time goes in v2:
time: 37.8 us; the launch traced here: 37.7 us
  Pallas kernels  36 us (95%)
  local copies, waits for them, and re-layouts  1.62 us (4%)
    pallas_call x1, Pallas kernels, per_device(): pl.pallas_call(functools.partial(kernel, sz, counts, capacity), out_shape...  36 us
    unnamed x1, local copies, waits for them, and re-layouts  1.62 us

profile of v2, /device:TPU:0, one launch (start us, length us, event | category | flops | bytes accessed | tf_op | source)
XLA Modules:
  0.0 37.7 jit_solution(9090392132804894646)
XLA Ops:
  0.0 36.0 %substeps.1 = f32[16,3072]{1,0:T(8,128)} custom-call(s32[3,2,2048]{2,1,0:T(2,128)} %bitcast.6, f32[3,2,2048]{2,1,0:T(2,128)} %bitcast.7, f32[3,2048]{1,0:T(4,128)} %refs_2_.1, f32[9,2048]{1,0:T(8,128)} %refs_3_.1, f32[1,2048]{1,0:T(1,128)} %bitcast.8, s32[512,128]{1,0:T(8,128)} %bitcast.5, s32[1,2048]{1,0:T(1,128)} %bitcast.9), custom_call_target="tpu_custom_call" | custom-call | tf_op jit(solution)/shard_map/substeps/pallas_call | solution.py:653
  36.0 1.6 %copy.9 = f32[16,3072]{1,0:T(8,128)} copy(f32[16,3072]{1,0:T(8,128)} %substeps.1) | data formatting | bytes 393216
